TPU v7x, 32 devices: a whole 2x2x4 slice. The times are simulated.
32 devices in a mesh: groups: 2 (over y), expert: 8 (over z, core), tensor: 2 (over x).
Axes of the slice: x: 2, y: 2, z: 4, core: 2. Of those that a mesh axis runs over, the one named last changes fastest.
Arguments:
- queries: bfloat16 [512, 4096], P(('groups', 'expert')), parts along dimension 0, may hold values from -200 to 200
- own_kv: bfloat16 [512, 1024], P(('groups', 'expert')), parts along dimension 0, may hold values from -6 to 6
- prompt_cache: bfloat16 [16, 256, 1024], P(('groups', 'expert'), 'tensor'), parts along dimension 0, may hold values from -8 to 8
- prompt_len: int32 [16], P(('groups', 'expert')), parts along dimension 0, may hold values from 2 to 256
- token_prompt: int32 [512], P(('groups', 'expert')), parts along dimension 0, may hold values from 0 to 7, as said below
- residual: bfloat16 [512, 2048], P(('groups', 'expert')), parts along dimension 0, may hold values from -3 to 3
- out_weight: bfloat16 [4096, 2048], P('tensor', 'expert'), may hold values from -0.125 to 0.125
- route_ids: int32 [512, 8], P(('groups', 'expert')), parts along dimension 0, may hold values from 0 to 15, all different within a row; in each aligned block of 32 rows (0 to 31, 32 to 63, ...) at most 24 rows name the same one
- route_weights: float32 [512, 8], P(('groups', 'expert')), parts along dimension 0, may hold values from 0.05 to 0.3
- w_gate: bfloat16 [16, 2048, 1024], P('expert', None, 'tensor'), may hold values from -0.125 to 0.125
- w_up: bfloat16 [16, 2048, 1024], P('expert', None, 'tensor'), may hold values from -0.125 to 0.125
- w_down: bfloat16 [16, 1024, 2048], P('expert', 'tensor'), may hold values from -0.25 to 0.25
Outputs:
- mixed: bfloat16 [512, 2048], P(('groups', 'expert'), 'tensor'), parts along dimension 0
There are 2 independent parts, one for each index of `groups`. A program takes and returns all parts, laid end to end along the dimension named above; an argument that names none is the same for every part. Nothing has to cross between parts.
Inputs may be any that keep to these rules, and one draw needn't show every extreme that they name: `token_prompt`: each index of the expert axis holds 8 tokens of each of 4 prompts and none of the others; each prompt has tokens on exactly 4 indices. `route_ids`: A row names distinct experts. Within the 32 rows of one index of the expert axis no expert is named more than 24 times, and in some of these blocks one is named exactly 24 times.
All inputs are finite; a program needn't handle non-finite values.
Results may differ from a plain program's by a relative error of at most 0.015.
Values may be sent and summed in bfloat16 or wider, within the bound.
A program may use at most 64 MiB of HBM per device.

v0:
```python
import functools

import jax
import jax.numpy as jnp
from jax import lax
from jax.experimental import pallas as pl
from jax.experimental.pallas import tpu as pltpu
from jax.sharding import PartitionSpec as P

HD = 128


MASKED_SCORE = -1e30


def combined_all(x, axis, combine):
    everything = jax.tree.map(
        lambda part, kind: lax.all_gather(part.astype(kind), axis),
        x,
        jax.tree.map(lambda a: jnp.bfloat16 if a.dtype == jnp.float32 else a.dtype, x),
    )

    def take(k):
        return jax.tree.map(lambda part, own: part[k].astype(own.dtype), everything, x)

    return lax.fori_loop(
        1, lax.axis_size(axis), lambda k, so_far: combine(so_far, take(k)), take(0)
    )


def combine_parts(earlier, later):
    top_a, sum_a, value_a = earlier
    top_b, sum_b, value_b = later
    top_score = jnp.maximum(top_a, top_b)
    shrink_a = jnp.exp(top_a - top_score)
    shrink_b = jnp.exp(top_b - top_score)
    return (
        top_score,
        sum_a * shrink_a + sum_b * shrink_b,
        value_a * shrink_a[..., None] + value_b * shrink_b[..., None],
    )


def local(
    queries,
    own_kv,
    prompt_cache,
    prompt_len,
    token_prompt,
    residual,
    out_weight,
    route_ids,
    route_weights,
    w_gate,
    w_up,
    w_down,
):
    tokens = queries.shape[0]
    half_cols = own_kv.shape[1] // 2
    kv_heads = half_cols // HD
    head_count = queries.shape[1] // HD
    group_size = head_count // kv_heads
    score_scale = HD ** (-0.5)
    expert_groups = lax.axis_size("expert")
    fan_count = expert_groups // 2
    per_prompt = tokens // fan_count
    order = jnp.argsort(token_prompt, stable=True)
    inverse = jnp.argsort(order)
    held_prompts = token_prompt[order].reshape(fan_count, per_prompt)[:, 0]
    sorted_query = queries[order].reshape(fan_count, per_prompt, kv_heads, group_size, HD)
    sorted_own = own_kv[order]
    own_keys = sorted_own[:, :half_cols].reshape(fan_count, per_prompt, kv_heads, HD)
    own_values = (
        sorted_own[:, half_cols:].reshape(fan_count, per_prompt, kv_heads, HD).astype(jnp.float32)
    )
    own_score = (
        jnp.einsum("imgjd,imgd->imgj", sorted_query, own_keys, preferred_element_type=jnp.float32)
        * score_scale
    )
    tensor_pos = lax.axis_index("tensor")
    leading = tensor_pos == 0
    start_top = jnp.where(leading, own_score, MASKED_SCORE)
    start_sum = jnp.where(leading, jnp.ones_like(own_score), jnp.zeros_like(own_score))
    start_values = jnp.where(
        leading,
        jnp.broadcast_to(
            own_values[:, :, :, None, :], (fan_count, per_prompt, kv_heads, group_size, HD)
        ),
        0.0,
    )
    block_len = prompt_cache.shape[1]
    positions = tensor_pos * block_len + jnp.arange(block_len, dtype=jnp.int32)
    cache_piece = lax.all_gather(prompt_cache, "expert", axis=0, tiled=True)
    length_piece = lax.all_gather(prompt_len, "expert", axis=0, tiled=True)
    shard_count = cache_piece.shape[0]
    owners = jnp.arange(shard_count, dtype=jnp.int32)
    matched = owners[:, None] == held_prompts[None, :]
    match_half = matched.astype(jnp.bfloat16)
    match_full = matched.astype(jnp.float32)
    present = jnp.any(matched, 0)
    piece_query = jnp.einsum(
        "qi,imgjd->qmgjd", match_half, sorted_query, preferred_element_type=jnp.float32
    ).astype(jnp.bfloat16)
    key_rows = cache_piece[:, :, :half_cols].reshape(shard_count, block_len, kv_heads, HD)
    value_rows = (
        cache_piece[:, :, half_cols:]
        .reshape(shard_count, block_len, kv_heads, HD)
        .astype(jnp.float32)
    )
    inside = (positions[None, :] < length_piece[:, None])[:, None, None, None, :]
    score_rows = (
        jnp.einsum("qmgjd,qpgd->qmgjp", piece_query, key_rows, preferred_element_type=jnp.float32)
        * score_scale
    )
    score_rows = jnp.where(inside, score_rows, MASKED_SCORE)
    piece_top = jnp.max(score_rows, -1)
    weights = jnp.where(inside, jnp.exp(score_rows - piece_top[..., None]), 0.0)
    piece_sum = jnp.sum(weights, -1)
    piece_values = jnp.einsum(
        "qmgjp,qpgd->qmgjd", weights, value_rows, precision=lax.Precision.HIGHEST
    )
    group_top = jnp.einsum("qi,qmgj->imgj", match_full, piece_top, precision=lax.Precision.HIGHEST)
    group_top = jnp.where(present[:, None, None, None], group_top, MASKED_SCORE)
    group_sum = jnp.einsum("qi,qmgj->imgj", match_full, piece_sum, precision=lax.Precision.HIGHEST)
    group_values = jnp.einsum(
        "qi,qmgjd->imgjd", match_full, piece_values, precision=lax.Precision.HIGHEST
    )
    folded = combine_parts(
        (start_top, start_sum, start_values), (group_top, group_sum, group_values)
    )
    top_score, weight_sum, value_sum = combined_all(folded, "tensor", combine_parts)
    attn_sorted = (value_sum / weight_sum[..., None]).reshape(tokens, head_count * HD)
    attn = attn_sorted[inverse].astype(jnp.bfloat16)
    rows_here = out_weight.shape[0]
    attn_mine = lax.dynamic_slice_in_dim(attn, tensor_pos * rows_here, rows_here, 1)
    column_terms = jnp.dot(
        lax.all_gather(attn_mine, "expert", axis=0, tiled=True),
        out_weight,
        preferred_element_type=jnp.float32,
    )
    partials = lax.all_to_all(
        column_terms.astype(jnp.bfloat16), "expert", split_axis=0, concat_axis=1, tiled=True
    ).astype(column_terms.dtype)
    model_width = residual.shape[1]
    col_width = model_width // lax.axis_size("tensor")
    col_start = tensor_pos * col_width
    resid_cols = lax.dynamic_slice_in_dim(residual, col_start, col_width, 1)
    experts_here = w_gate.shape[0]
    experts = experts_here * expert_groups
    picks = route_ids.shape[1]
    capacity = min(tokens, 3 * tokens * picks // (2 * experts))
    flat_ids = route_ids.reshape(-1)
    expert_marks = (flat_ids[:, None] == jnp.arange(experts, dtype=jnp.int32)[None, :]).astype(
        jnp.int32
    )
    slot_index = jnp.sum((jnp.cumsum(expert_marks, 0) - expert_marks) * expert_marks, 1)
    destination = flat_ids * capacity + slot_index
    source_rows = jnp.arange(tokens * picks, dtype=jnp.int32) // picks
    head_total = lax.psum_scatter(
        partials.astype(jnp.bfloat16), "tensor", scatter_dimension=1, tiled=True
    ).astype(jnp.float32)
    hidden_cols = (resid_cols.astype(jnp.float32) + head_total).astype(jnp.bfloat16)
    outgoing = (
        jnp.zeros((experts * capacity, col_width), jnp.bfloat16)
        .at[destination]
        .set(hidden_cols[source_rows])
    )
    outgoing = outgoing.reshape(expert_groups, experts_here, capacity, col_width)
    arrived = lax.all_to_all(outgoing, "expert", split_axis=0, concat_axis=0, tiled=True)
    arrived = lax.all_gather(arrived, "tensor", axis=3, tiled=True)
    gate_proj = jnp.einsum("sxcd,xdf->sxcf", arrived, w_gate, preferred_element_type=jnp.float32)
    up_proj = jnp.einsum("sxcd,xdf->sxcf", arrived, w_up, preferred_element_type=jnp.float32)
    activated = (jax.nn.silu(gate_proj) * up_proj).astype(jnp.bfloat16)
    expert_partials = jnp.einsum(
        "sxcf,xfd->sxcd", activated, w_down, preferred_element_type=jnp.float32
    )
    summed = lax.psum_scatter(
        expert_partials.astype(jnp.bfloat16), "tensor", scatter_dimension=3, tiled=True
    )
    returned = lax.all_to_all(summed, "expert", split_axis=0, concat_axis=0, tiled=True).reshape(
        experts * capacity, col_width
    )
    picked = returned[destination].reshape(tokens, picks, col_width).astype(jnp.float32)
    expert_mix = jnp.sum(route_weights[:, :, None] * picked, 1)
    return (hidden_cols.astype(jnp.float32) + expert_mix).astype(jnp.bfloat16)


F32 = jnp.float32
BF16 = jnp.bfloat16
MESH = pl.DeviceIdType.MESH


def dot(a, b):
    return jnp.dot(a, b, preferred_element_type=F32)


def iota(shape, dim):
    return lax.broadcasted_iota(jnp.int32, shape, dim)


def fused_kernel(
    sizes,
    queries,
    own_kv,
    cache,
    length,
    tp_row,
    residual,
    ids,
    route_w,
    wo_hbm,
    wg_hbm,
    wu_hbm,
    wd_hbm,
    out,
    wo,
    wg,
    wu,
    wd,
    qsend,
    qrecv,
    kv,
    msend,
    meta,
    resid,
    attn,
    ybuf,
    yrecv,
    hidden,
    act,
    total,
    dsend,
    drecv,
    xsend,
    xrecv,
    zsend,
    zrecv,
    w_sem,
    q_ss,
    q_rs,
    m_ss,
    m_rs,
    r_ss,
    r_rs,
    k_ss,
    k_rs,
    a_ss,
    a_rs,
    y_ss,
    y_rs,
    h_ss,
    h_rs,
    d_ss,
    d_rs,
    x_ss,
    x_rs,
    z_ss,
    z_rs,
):
    n, tokens, per, kvl, group = sizes
    nz = n // 2
    me = lax.axis_index("expert")
    t = lax.axis_index("tensor")
    ot = 1 - t
    z = me // 2
    c = lax.rem(me, 2)
    mate = z * 2 + 1 - c
    everyone = n * tokens
    model = residual.shape[1]
    cols = model // n
    hc = cols // 2
    half = model // 2
    heads_cols = kvl * group * HD
    block_cols = group * HD + 2 * HD
    half_kv = own_kv.shape[1] // 2
    experts_here = wg.shape[0]
    ff = wg.shape[2]

    def peer(k):
        return lax.rem(me + k, n)

    def zpeer(k):
        return lax.rem(z + k, nz) * 2 + c

    def mult(x, m):
        return pl.multiple_of(x, m)

    loads = [
        pltpu.make_async_copy(a, b, w_sem.at[i])
        for i, (a, b) in enumerate(((wo_hbm, wo), (wg_hbm, wg), (wu_hbm, wu), (wd_hbm, wd)))
    ]
    for load in loads:
        load.start()

    barrier = pltpu.get_barrier_semaphore()
    for k in range(1, n):
        pl.semaphore_signal(
            barrier, inc=1, device_id={"expert": peer(k), "tensor": t}, device_id_type=MESH
        )
    pl.semaphore_signal(
        barrier, inc=1, device_id={"expert": me, "tensor": ot}, device_id_type=MESH
    )

    def remote(src, dst, ss, rs, e, tt):
        return pltpu.make_async_remote_copy(
            src_ref=src,
            dst_ref=dst,
            send_sem=ss,
            recv_sem=rs,
            device_id={"expert": e, "tensor": tt},
            device_id_type=MESH,
        )

    marked = (iota((n, tokens), 0) == tp_row[...]).astype(F32)
    before = (iota((tokens, tokens), 0) < iota((tokens, tokens), 1)).astype(F32)
    counted = dot(marked.astype(BF16), before.astype(BF16)) * marked
    rank_row = jnp.sum(counted, axis=0, keepdims=True).astype(jnp.int32)
    shape = (n * kvl * per, tokens)
    at = iota(shape, 0)
    hit = (at // (kvl * per) == tp_row[...]) & (lax.rem(at, per) == rank_row)
    spread = []
    for g in range(kvl):
        mark = (hit & (lax.rem(at // per, kvl) == g)).astype(F32).astype(BF16)
        spread.append(mark)
    q_parts = k_parts = v_parts = None
    for g in range(kvl):
        head = t * kvl + g
        q_part = dot(
            spread[g], queries[:, pl.ds(mult(head * group * HD, group * HD), group * HD)]
        )
        k_part = dot(spread[g], own_kv[:, pl.ds(mult(head * HD, HD), HD)])
        v_part = dot(spread[g], own_kv[:, pl.ds(mult(half_kv + head * HD, HD), HD)])
        q_parts = q_part if g == 0 else q_parts + q_part
        k_parts = k_part if g == 0 else k_parts + k_part
        v_parts = v_part if g == 0 else v_parts + v_part
    block = (n, kvl * per, HD)
    qsend[:, :, 0 : group * HD] = q_parts.astype(BF16).reshape(n, kvl * per, group * HD)
    qsend[:, :, group * HD : group * HD + HD] = k_parts.astype(BF16).reshape(block)
    qsend[:, :, group * HD + HD : block_cols] = v_parts.astype(BF16).reshape(block)

    lanes = meta.shape[2]
    at = iota((n * 8, tokens), 0)
    row = lax.rem(at, 8)
    wanted = jnp.where(row < experts_here, at // 8 * experts_here + row, -1)
    facts = jnp.where(row == experts_here, tp_row[...].astype(F32), 0.0)
    for k in range(ids.shape[0]):
        facts = facts + jnp.where(wanted == ids[k : k + 1, :], route_w[k : k + 1, :], 0.0)
    facts = jnp.concatenate([facts, jnp.zeros((n * 8, lanes - tokens), F32)], axis=1)
    msend[...] = facts.reshape(n, 8, lanes)

    pl.semaphore_wait(barrier, n)

    sends = []

    def go(copy):
        copy.start()
        sends.append(copy)

    for k in range(1, n):
        e = peer(k)
        go(remote(qsend.at[e], qrecv.at[me], q_ss.at[k], q_rs.at[me], e, t))
        go(remote(msend.at[e], meta.at[me], m_ss.at[k], m_rs.at[me], e, t))
    kvw = kvl * HD
    span = cache.shape[1]
    for i in range(2):
        go(
            remote(
                cache.at[0, :, pl.ds(mult(i * half_kv + ot * kvw, kvw), kvw)],
                kv.at[pl.ds(mult(t * span, span), span), pl.ds(i * kvw, kvw)],
                k_ss.at[i],
                k_rs.at[i],
                me,
                ot,
            )
        )
    for k in range(1, n):
        e = peer(k)
        go(
            remote(
                residual.at[:, pl.ds(mult(e * cols + t * hc, hc), hc)],
                resid.at[me],
                r_ss.at[k],
                r_rs.at[me],
                e,
                t,
            )
        )

    qrecv[me] = qsend[me]
    meta[me] = msend[me]
    resid[me] = residual[:, pl.ds(mult(me * cols + t * hc, hc), hc)]
    for i in range(2):
        kv[pl.ds(mult(t * span, span), span), i * kvw : (i + 1) * kvw] = cache[
            0, :, pl.ds(mult(i * half_kv + t * kvw, kvw), kvw)
        ]

    for k in range(1, n):
        e = peer(k)
        remote(meta.at[e], meta.at[e], m_ss.at[k], m_rs.at[e], e, t).wait_recv()

    slots = n * kvl * per
    place = iota((tokens, slots), 1)
    j = iota((tokens, slots), 0)
    base = jnp.zeros((1, 1), jnp.int32)
    pick = jnp.zeros((tokens, slots), F32)
    for s in range(n):
        names = meta[s, experts_here : experts_here + 1, 0:tokens].astype(jnp.int32)
        found = jnp.max((names == me).astype(F32), axis=1, keepdims=True)
        fits = (place // (kvl * per) == s) & (j == base + lax.rem(place, per))
        pick = pick + jnp.where(fits, found, 0.0)
        base = base + (found * per).astype(jnp.int32)
    for k in range(1, n):
        e = peer(k)
        remote(qsend.at[e], qrecv.at[e], q_ss.at[k], q_rs.at[e], e, t).wait_recv()
    for i in range(2):
        part = kv.at[pl.ds(mult(ot * span, span), span), pl.ds(i * kvw, kvw)]
        remote(part, part, k_ss.at[i], k_rs.at[i], me, ot).wait_recv()

    got = qrecv[...].reshape(slots, block_cols)
    positions = kv.shape[0]
    scale = HD ** (-0.5)
    inside = iota((1, positions), 1) < length[...]
    for g in range(kvl):
        chosen_rows = jnp.where(lax.rem(place // per, kvl) == g, pick, 0.0).astype(BF16)
        mine = dot(chosen_rows, got)
        q = jnp.concatenate([mine[:, i * HD : (i + 1) * HD] for i in range(group)], 0)
        k_own = jnp.concatenate([mine[:, group * HD : group * HD + HD]] * group, 0)
        v_own = jnp.concatenate([mine[:, group * HD + HD : block_cols]] * group, 0)
        keys = kv[:, g * HD : (g + 1) * HD]
        values = kv[:, kvw + g * HD : kvw + (g + 1) * HD]
        score = (
            lax.dot_general(
                q.astype(BF16), keys, (((1,), (1,)), ((), ())), preferred_element_type=F32
            )
            * scale
        )
        score = jnp.where(inside, score, MASKED_SCORE)
        own_score = jnp.sum(q * k_own, axis=1, keepdims=True) * scale
        top = jnp.maximum(jnp.max(score, axis=1, keepdims=True), own_score)
        weight = jnp.where(inside, jnp.exp(score - top), 0.0)
        own_weight = jnp.exp(own_score - top)
        bottom = jnp.sum(weight, axis=1, keepdims=True) + own_weight
        value = (dot(weight.astype(BF16), values) + own_weight * v_own) / bottom
        value = value.astype(BF16)
        for i in range(group):
            at_col = (g * group + i) * HD
            attn[me, :, at_col : at_col + HD] = value[i * tokens : (i + 1) * tokens]

    def gather_start(buf, ss, rs):
        for k in range(1, nz):
            go(remote(buf.at[me], buf.at[me], ss.at[k], rs.at[me], zpeer(k), t))
        go(remote(buf.at[me], buf.at[me], ss.at[0], rs.at[me], mate, t))

    def gather_take(buf, ss, rs, use):
        use(me)
        remote(buf.at[mate], buf.at[mate], ss.at[0], rs.at[mate], mate, t).wait_recv()
        use(mate)
        for k in range(1, nz):
            b = zpeer(k)
            remote(buf.at[b], buf.at[b], ss.at[0], rs.at[b], mate, t).wait_recv()
            go(remote(buf.at[b], buf.at[b], ss.at[nz - 1 + k], rs.at[b], mate, t))
            use(b)
        for k in range(1, nz):
            b = lax.rem(z + k, nz) * 2 + 1 - c
            remote(buf.at[b], buf.at[b], ss.at[0], rs.at[b], mate, t).wait_recv()
            use(b)

    gather_start(attn, a_ss, a_rs)

    for k in range(1, n):
        e = peer(k)
        remote(resid.at[e], resid.at[e], r_ss.at[k], r_rs.at[e], e, t).wait_recv()
    info = meta[...].reshape(n * 8, lanes).T

    def column(r):
        return jnp.concatenate(
            [info[0:tokens, i * 8 + r : i * 8 + r + 1] for i in range(n)], axis=0
        )

    prompt = column(experts_here)
    wide = iota((everyone, lanes), 1)
    named = (prompt.astype(jnp.int32) == wide).astype(F32)
    square = (everyone, everyone)
    earlier = (iota(square, 1) < iota(square, 0)).astype(F32).astype(BF16)
    rank = jnp.sum(dot(earlier, named.astype(BF16)) * named, axis=1, keepdims=True)
    row_at = (prompt * tokens + rank).astype(jnp.int32)
    unsort = (row_at == iota(square, 1)).astype(F32).astype(BF16)
    mixes = [column(x) for x in range(experts_here)]

    gather_take(attn, a_ss, a_rs, lambda b: None)
    loads[0].wait()
    y = dot(attn[...].reshape(everyone, heads_cols), wo[...]).astype(BF16)
    ybuf[...] = dot(unsort, y).astype(BF16)
    there = pl.ds(mult(ot * hc, hc), hc)
    here = pl.ds(mult(t * hc, hc), hc)
    y_copy = remote(ybuf.at[:, there], yrecv, y_ss.at[0], y_rs.at[0], me, ot)
    go(y_copy)
    y_copy.wait_recv()
    hid = resid[...].reshape(everyone, hc).astype(F32) + (
        ybuf[:, here].astype(F32) + yrecv[...].astype(F32)
    )
    hidden[:, pl.ds(mult(me * cols + t * hc, hc), hc)] = hid.astype(BF16)

    def pass_on(b, half_at, k, e, tt):
        part = hidden.at[:, pl.ds(mult(b * cols + half_at * hc, hc), hc)]
        go(remote(part, part, h_ss.at[k], h_rs.at[2 * b + half_at], e, tt))

    def arrives(b, half_at):
        part = hidden.at[:, pl.ds(mult(b * cols + half_at * hc, hc), hc)]
        remote(part, part, h_ss.at[0], h_rs.at[2 * b + half_at], mate, t).wait_recv()

    for k in range(1, nz):
        pass_on(me, t, k, zpeer(k), t)
    pass_on(me, t, nz, me, ot)
    pass_on(me, t, 0, mate, t)
    for k in range(1, nz):
        b = zpeer(k)
        arrives(b, t)
        pass_on(b, t, nz + k, me, ot)
        pass_on(b, t, 2 * nz + k, mate, t)
    for k in range(nz):
        b = zpeer(k)
        arrives(b, ot)
        pass_on(b, ot, 3 * nz + k, mate, t)
    for k in range(nz):
        other = lax.rem(z + k, nz) * 2 + 1 - c
        arrives(other, t)
        arrives(other, ot)
    loads[1].wait()
    loads[2].wait()
    for x in range(experts_here):
        gate = dot(hidden[...], wg[x])
        value = gate / (1.0 + jnp.exp(-gate)) * dot(hidden[...], wu[x]) * mixes[x]
        act[:, x * ff : (x + 1) * ff] = value.astype(BF16)
    loads[3].wait()

    order = [*range(1, nz), 0]

    def down(side, at_sem):
        at_cols = pl.ds(mult(side * half, half), half)
        part = None
        for x in range(experts_here):
            term = dot(act[:, x * ff : (x + 1) * ff], wd[x, :, at_cols])
            part = term if part is None else part + term
        total[:, at_cols] = part
        for k in order:
            zz = lax.rem(z + k, nz)
            theirs = pl.ds(mult((zz * 2 + 1 - c) * tokens, tokens), tokens)
            dsend[zz, :, at_cols] = total[theirs, at_cols].astype(BF16)
            moved = dsend.at[zz, :, at_cols]
            dest = drecv.at[zz, :, at_cols]
            go(remote(moved, dest, d_ss.at[at_sem + k], d_rs.at[at_sem + zz], mate, t))

    def from_mate(side, at_sem, k, zz):
        at_cols = pl.ds(mult(side * half, half), half)
        dest = drecv.at[zz, :, at_cols]
        remote(dest, dest, d_ss.at[at_sem + k], d_rs.at[at_sem + zz], mate, t).wait_recv()

    down(ot, 0)
    there = pl.ds(mult(ot * half, half), half)
    here = pl.ds(mult(t * half, half), half)
    for k in order:
        zz = lax.rem(z + k, nz)
        from_mate(ot, 0, k, zz)
        ours = pl.ds(mult((zz * 2 + c) * tokens, tokens), tokens)
        xsend[zz] = (total[ours, there] + drecv[zz, :, there].astype(F32)).astype(BF16)
        go(remote(xsend.at[zz], xrecv.at[zz], x_ss.at[k], x_rs.at[zz], me, ot))
    down(t, nz)
    for k in order:
        zz = lax.rem(z + k, nz)
        from_mate(t, nz, k, zz)
        remote(xsend.at[zz], xrecv.at[zz], x_ss.at[k], x_rs.at[zz], me, ot).wait_recv()
        ours = pl.ds(mult((zz * 2 + c) * tokens, tokens), tokens)
        done = total[ours, here] + drecv[zz, :, here].astype(F32) + xrecv[zz].astype(F32)
        if k:
            zsend[zz] = done.astype(BF16)
            go(remote(zsend.at[zz], zrecv.at[z], z_ss.at[k], z_rs.at[z], zz * 2 + c, t))
        else:
            total[ours, here] = done
    own_rows = pl.ds(mult(me * tokens, tokens), tokens)
    final = total[own_rows, pl.ds(mult(t * half, half), half)]
    final = final + hidden[own_rows, here].astype(F32)
    for k in range(1, nz):
        zz = lax.rem(z + k, nz)
        remote(zsend.at[zz], zrecv.at[zz], z_ss.at[k], z_rs.at[zz], zz * 2 + c, t).wait_recv()
        final = final + zrecv[zz].astype(F32)
    out[...] = final.astype(BF16)
    for copy in sends:
        copy.wait_send()


def fused(
    queries,
    own_kv,
    prompt_cache,
    prompt_len,
    token_prompt,
    residual,
    out_weight,
    route_ids,
    route_weights,
    w_gate,
    w_up,
    w_down,
):
    n = lax.axis_size("expert")
    nz = n // 2
    tokens = queries.shape[0]
    per = tokens // nz
    kv_heads = own_kv.shape[1] // (2 * HD)
    group = queries.shape[1] // HD // kv_heads
    kvl = kv_heads // 2
    model = residual.shape[1]
    cols = model // n
    hc = cols // 2
    half = model // 2
    rows_per = kvl * per
    block_cols = group * HD + 2 * HD
    x_here, _, ff = w_gate.shape
    every = n * tokens
    sem = pltpu.SemaphoreType.DMA

    def vm(shape, kind=BF16):
        return pltpu.VMEM(shape, kind)

    vspec = pl.BlockSpec(memory_space=pltpu.VMEM)
    hspec = pl.BlockSpec(memory_space=pl.ANY)
    return pl.pallas_call(
        functools.partial(fused_kernel, (n, tokens, per, kvl, group)),
        out_shape=jax.ShapeDtypeStruct((tokens, half), BF16),
        in_specs=[vspec] * 8 + [hspec] * 4,
        out_specs=vspec,
        scratch_shapes=[
            vm(out_weight.shape),
            vm(w_gate.shape),
            vm(w_up.shape),
            vm(w_down.shape),
            vm((n, rows_per, block_cols)),
            vm((n, rows_per, block_cols)),
            vm((2 * prompt_cache.shape[1], 2 * kvl * HD)),
            vm((n, 8, HD), F32),
            vm((n, 8, HD), F32),
            vm((n, tokens, cols // 2)),
            vm((n, tokens, kvl * group * HD)),
            vm((every, cols)),
            vm((every, cols // 2)),
            vm((every, model)),
            vm((every, x_here * ff)),
            vm((every, model), F32),
            vm((nz, tokens, model)),
            vm((nz, tokens, model)),
            vm((nz, tokens, half)),
            vm((nz, tokens, half)),
            vm((nz, tokens, half)),
            vm((nz, tokens, half)),
            sem((4,)),
            sem((n,)),
            sem((n,)),
            sem((n,)),
            sem((n,)),
            sem((n,)),
            sem((n,)),
            sem((2,)),
            sem((2,)),
            sem((2 * nz,)),
            sem((n,)),
            sem((1,)),
            sem((1,)),
            sem((4 * nz,)),
            sem((2 * n,)),
            sem((2 * nz,)),
            sem((2 * nz,)),
            sem((nz,)),
            sem((nz,)),
            sem((nz,)),
            sem((nz,)),
        ],
        compiler_params=pltpu.CompilerParams(
            collective_id=0, has_side_effects=True, vmem_limit_bytes=60 * 1024 * 1024
        ),
    )(
        queries,
        own_kv,
        prompt_cache,
        prompt_len.reshape(1, 1),
        token_prompt.reshape(1, tokens),
        residual,
        route_ids.T,
        route_weights.T,
        out_weight,
        w_gate,
        w_up,
        w_down,
    )


def chosen(*arrays):
    queries, own_kv, _, _, _, residual, _, _, _, w_gate, _, _ = arrays
    n = lax.axis_size("expert")
    tokens = queries.shape[0]
    kv_heads = own_kv.shape[1] // (2 * HD)
    fits = (
        lax.axis_size("tensor") == 2
        and n % 2 == 0
        and tokens % 16 == 0
        and tokens <= HD
        and tokens % (n // 2) == 0
        and kv_heads % 2 == 0
        and (kv_heads // 2) * (tokens // (n // 2)) % 16 == 0
        and residual.shape[1] % (2 * n * HD) == 0
        and w_gate.shape[0] < 8
        and 6 * w_gate.size + 24 * n * tokens * residual.shape[1] < 50 * 2**20
    )
    return fused(*arrays) if fits else local(*arrays)


def solution(mesh):
    in_specs = (
        P(("groups", "expert"), None),
        P(("groups", "expert"), None),
        P(("groups", "expert"), "tensor", None),
        P(("groups", "expert")),
        P(("groups", "expert")),
        P(("groups", "expert"), None),
        P("tensor", "expert"),
        P(("groups", "expert"), None),
        P(("groups", "expert"), None),
        P("expert", None, "tensor"),
        P("expert", None, "tensor"),
        P("expert", "tensor", None),
    )
    out_specs = P(("groups", "expert"), "tensor")
    return jax.shard_map(chosen, mesh=mesh, in_specs=in_specs, out_specs=out_specs, check_vma=False)
```

profile of v0, /device:TPU:0, one launch (start us, length us, event | category | flops | bytes accessed | tf_op | source)
XLA Modules:
  0.0 66.4 jit_solution(18166887070402739457)
XLA Ops:
  0.7 64.3 %shard_map.118 = bf16[32,1024]{1,0:T(8,128)(2,1)} custom-call(bf16[32,4096]{1,0:T(8,128)(2,1)} %queries.1, bf16[32,1024]{1,0:T(8,128)(2,1)} %own_kv.1, bf16[1,128,1024]{2,1,0:T(8,128)(2,1)} %cache.1, s32[1,1]{1,0:T(1,128)} %bitcast.4.length, s32[1,32]{1,0:T(1,128)} %bitcast.7, bf16[32,2048]{1,0:T(8,128)(2,1)} %residual.1, s32[8,32]{1,0:T(8,128)} %bitcast.5, ...), custom_call_target="tpu_custom_call" | custom-call | tf_op jit(solution)/shard_map/pallas_call | solution.py:628
  64.9 1.5 %copy.15 = bf16[32,1024]{1,0:T(8,128)(2,1)} copy(bf16[32,1024]{1,0:T(8,128)(2,1)} %shard_map.118) | data formatting | bytes 131072
where the time goes:
time: 66.6 us; the launch traced here: 66.4 us
  Pallas kernels  64.3 us (97%)
  local copies, waits for them, and re-layouts  1.47 us (2%)
    pallas_call x1, Pallas kernels, fused(): pl.pallas_call(functools.partial(fused_kernel, (n, tokens, per, kvl, grou...  64.3 us
    unnamed x1, local copies, waits for them, and re-layouts  1.47 us

commit v1 on v0

--- a/solution.py
+++ b/solution.py
@@ -200,19 +200,25 @@
 
 def fused_kernel(
     sizes,
-    queries,
-    own_kv,
+    queries_hbm,
+    own_kv_hbm,
     cache,
-    length,
-    tp_row,
+    length_hbm,
+    tp_hbm,
     residual,
-    ids,
-    route_w,
+    ids_hbm,
+    route_w_hbm,
     wo_hbm,
     wg_hbm,
     wu_hbm,
     wd_hbm,
     out,
+    queries,
+    own_kv,
+    length,
+    tp_row,
+    ids,
+    route_w,
     wo,
     wg,
     wu,
@@ -223,11 +229,15 @@
     msend,
     meta,
     resid,
+    sorted_resid,
+    perm,
+    mixes,
     attn,
     ybuf,
     yrecv,
     hidden,
     act,
+    own_act,
     total,
     dsend,
     drecv,
@@ -235,6 +245,7 @@
     xrecv,
     zsend,
     zrecv,
+    in_sem,
     w_sem,
     q_ss,
     q_rs,
@@ -246,6 +257,8 @@
     k_rs,
     a_ss,
     a_rs,
+    m_up_ss,
+    m_up_rs,
     y_ss,
     y_rs,
     h_ss,
@@ -276,11 +289,19 @@
     experts_here = wg.shape[0]
     ff = wg.shape[2]
 
+    step = 2 * (z // (nz // 2)) - 1
+
+    def zline(k):
+        return lax.rem(z + nz + step * k, nz)
+
     def peer(k):
-        return lax.rem(me + k, n)
+        return zline(k // 2) * 2 + lax.rem(c + k, 2)
 
     def zpeer(k):
-        return lax.rem(z + k, nz) * 2 + c
+        return zline(k) * 2 + c
+
+    def slot(b):
+        return lax.rem(b + n - 2, n)
 
     def mult(x, m):
         return pl.multiple_of(x, m)
@@ -289,8 +310,21 @@
         pltpu.make_async_copy(a, b, w_sem.at[i])
         for i, (a, b) in enumerate(((wo_hbm, wo), (wg_hbm, wg), (wu_hbm, wu), (wd_hbm, wd)))
     ]
-    for load in loads:
-        load.start()
+    fetched = [
+        pltpu.make_async_copy(a, b, in_sem.at[i])
+        for i, (a, b) in enumerate(
+            (
+                (tp_hbm, tp_row),
+                (queries_hbm, queries),
+                (own_kv_hbm, own_kv),
+                (ids_hbm, ids),
+                (route_w_hbm, route_w),
+                (length_hbm, length),
+            )
+        )
+    ]
+    for fetch in fetched:
+        fetch.start()
 
     barrier = pltpu.get_barrier_semaphore()
     for k in range(1, n):
@@ -311,6 +345,25 @@
             device_id_type=MESH,
         )
 
+    kvw = kvl * HD
+    span = cache.shape[1]
+    mine_at = pl.ds(mult(t * span, span), span)
+    own_half = [
+        pltpu.make_async_copy(
+            cache.at[0, :, pl.ds(mult(i * half_kv + t * kvw, kvw), kvw)],
+            kv.at[mine_at, pl.ds(i * kvw, kvw)],
+            in_sem.at[6 + i],
+        )
+        for i in range(2)
+    ]
+    own_half.append(
+        pltpu.make_async_copy(
+            residual.at[:, pl.ds(mult(me * cols + t * hc, hc), hc)], resid.at[me], in_sem.at[8]
+        )
+    )
+    for load in own_half:
+        load.start()
+    fetched[0].wait()
     marked = (iota((n, tokens), 0) == tp_row[...]).astype(F32)
     before = (iota((tokens, tokens), 0) < iota((tokens, tokens), 1)).astype(F32)
     counted = dot(marked.astype(BF16), before.astype(BF16)) * marked
@@ -322,6 +375,8 @@
     for g in range(kvl):
         mark = (hit & (lax.rem(at // per, kvl) == g)).astype(F32).astype(BF16)
         spread.append(mark)
+    fetched[1].wait()
+    fetched[2].wait()
     q_parts = k_parts = v_parts = None
     for g in range(kvl):
         head = t * kvl + g
@@ -338,6 +393,8 @@
     qsend[:, :, group * HD : group * HD + HD] = k_parts.astype(BF16).reshape(block)
     qsend[:, :, group * HD + HD : block_cols] = v_parts.astype(BF16).reshape(block)
 
+    fetched[3].wait()
+    fetched[4].wait()
     lanes = meta.shape[2]
     at = iota((n * 8, tokens), 0)
     row = lax.rem(at, 8)
@@ -356,17 +413,15 @@
         copy.start()
         sends.append(copy)
 
-    for k in range(1, n):
+    for k in [*range(2, n), 1]:
         e = peer(k)
         go(remote(qsend.at[e], qrecv.at[me], q_ss.at[k], q_rs.at[me], e, t))
         go(remote(msend.at[e], meta.at[me], m_ss.at[k], m_rs.at[me], e, t))
-    kvw = kvl * HD
-    span = cache.shape[1]
     for i in range(2):
         go(
             remote(
                 cache.at[0, :, pl.ds(mult(i * half_kv + ot * kvw, kvw), kvw)],
-                kv.at[pl.ds(mult(t * span, span), span), pl.ds(i * kvw, kvw)],
+                kv.at[mine_at, pl.ds(i * kvw, kvw)],
                 k_ss.at[i],
                 k_rs.at[i],
                 me,
@@ -388,11 +443,11 @@
 
     qrecv[me] = qsend[me]
     meta[me] = msend[me]
-    resid[me] = residual[:, pl.ds(mult(me * cols + t * hc, hc), hc)]
-    for i in range(2):
-        kv[pl.ds(mult(t * span, span), span), i * kvw : (i + 1) * kvw] = cache[
-            0, :, pl.ds(mult(i * half_kv + t * kvw, kvw), kvw)
-        ]
+    for load in loads:
+        load.start()
+    for load in own_half:
+        load.wait()
+    fetched[5].wait()
 
     for k in range(1, n):
         e = peer(k)
@@ -416,6 +471,37 @@
         part = kv.at[pl.ds(mult(ot * span, span), span), pl.ds(i * kvw, kvw)]
         remote(part, part, k_ss.at[i], k_rs.at[i], me, ot).wait_recv()
 
+    quarters = 2 * kvl
+    quarter = heads_cols // quarters
+    predicated = []
+
+    def inside_line(zz):
+        return (zz >= 0) & (zz < nz)
+
+    def line_copy(off, q, way, at):
+        b = (z + off) * 2 + c
+        part = attn.at[slot(b), :, pl.ds(q * quarter, quarter)]
+        return remote(
+            part, part, a_ss.at[at], a_rs.at[slot(b) * quarters + q], (z + way) * 2 + c, t
+        )
+
+    def pass_line(off, q, way, at):
+        pl.when(inside_line(z + way))(lambda: line_copy(off, q, way, at).start())
+        predicated.append((off, way, functools.partial(line_copy, off, q, way, at)))
+
+    def arrived(off, q):
+        line_copy(off, q, 0, 0).wait_recv()
+
+    def mate_copy(off, at):
+        block = attn.at[slot((z + off) * 2 + c)]
+        return remote(
+            block, block, m_up_ss.at[at], m_up_rs.at[slot((z + off) * 2 + c)], mate, t
+        )
+
+    def to_mate(off, at):
+        mate_copy(off, at).start()
+        predicated.append((off, 0, functools.partial(mate_copy, off, at)))
+
     got = qrecv[...].reshape(slots, block_cols)
     positions = kv.shape[0]
     scale = HD ** (-0.5)
@@ -444,32 +530,12 @@
         value = value.astype(BF16)
         for i in range(group):
             at_col = (g * group + i) * HD
-            attn[me, :, at_col : at_col + HD] = value[i * tokens : (i + 1) * tokens]
-
-    def gather_start(buf, ss, rs):
-        for k in range(1, nz):
-            go(remote(buf.at[me], buf.at[me], ss.at[k], rs.at[me], zpeer(k), t))
-        go(remote(buf.at[me], buf.at[me], ss.at[0], rs.at[me], mate, t))
-
-    def gather_take(buf, ss, rs, use):
-        use(me)
-        remote(buf.at[mate], buf.at[mate], ss.at[0], rs.at[mate], mate, t).wait_recv()
-        use(mate)
-        for k in range(1, nz):
-            b = zpeer(k)
-            remote(buf.at[b], buf.at[b], ss.at[0], rs.at[b], mate, t).wait_recv()
-            go(remote(buf.at[b], buf.at[b], ss.at[nz - 1 + k], rs.at[b], mate, t))
-            use(b)
-        for k in range(1, nz):
-            b = lax.rem(z + k, nz) * 2 + 1 - c
-            remote(buf.at[b], buf.at[b], ss.at[0], rs.at[b], mate, t).wait_recv()
-            use(b)
-
-    gather_start(attn, a_ss, a_rs)
-
-    for k in range(1, n):
-        e = peer(k)
-        remote(resid.at[e], resid.at[e], r_ss.at[k], r_rs.at[e], e, t).wait_recv()
+            attn[slot(me), :, at_col : at_col + HD] = value[i * tokens : (i + 1) * tokens]
+        for q in range(g * quarters // kvl, (g + 1) * quarters // kvl):
+            pass_line(0, q, -1, q)
+            pass_line(0, q, 1, quarters + q)
+    to_mate(0, 0)
+
     info = meta[...].reshape(n * 8, lanes).T
 
     def column(r):
@@ -483,110 +549,210 @@
     square = (everyone, everyone)
     earlier = (iota(square, 1) < iota(square, 0)).astype(F32).astype(BF16)
     rank = jnp.sum(dot(earlier, named.astype(BF16)) * named, axis=1, keepdims=True)
-    row_at = (prompt * tokens + rank).astype(jnp.int32)
-    unsort = (row_at == iota(square, 1)).astype(F32).astype(BF16)
-    mixes = [column(x) for x in range(experts_here)]
-
-    gather_take(attn, a_ss, a_rs, lambda b: None)
-    loads[0].wait()
-    y = dot(attn[...].reshape(everyone, heads_cols), wo[...]).astype(BF16)
-    ybuf[...] = dot(unsort, y).astype(BF16)
+    shifted = prompt + jnp.where(prompt < 2, n - 2, -2).astype(F32)
+    row_at = (shifted * tokens + rank).astype(jnp.int32)
+    chosen_at = (row_at == iota(square, 1)).astype(F32)
+    perm[...] = chosen_at.astype(BF16)
+    to_sorted = chosen_at.T.astype(BF16)
+    spread_mix = jnp.zeros((everyone, lanes), F32)
+    for x in range(experts_here):
+        left = column(x)
+        for i in range(3):
+            piece = left.astype(BF16).astype(F32)
+            left = left - piece
+            spread_mix = spread_mix + jnp.where(wide == 3 * x + i, piece, 0.0)
+    mixes[...] = dot(to_sorted, spread_mix.astype(BF16))
+
+    def take(d):
+        for q in range(quarters):
+            for way in (1, -1):
+
+                def land(q=q, way=way):
+                    arrived(-way * d, q)
+                    pass_line(-way * d, q, way, 2 * quarters * d + (quarters if way > 0 else 0) + q)
+
+                pl.when(inside_line(z - way * d))(land)
+        for way in (1, -1):
+
+            def hand(way=way):
+                to_mate(-way * d, 2 * d + (1 if way > 0 else 0))
+
+            pl.when(inside_line(z - way * d))(hand)
+
+    rows_a = (n - 4) * tokens
+    stages = [(0, rows_a), (rows_a, everyone)]
     there = pl.ds(mult(ot * hc, hc), hc)
     here = pl.ds(mult(t * hc, hc), hc)
-    y_copy = remote(ybuf.at[:, there], yrecv, y_ss.at[0], y_rs.at[0], me, ot)
-    go(y_copy)
-    y_copy.wait_recv()
-    hid = resid[...].reshape(everyone, hc).astype(F32) + (
-        ybuf[:, here].astype(F32) + yrecv[...].astype(F32)
-    )
-    hidden[:, pl.ds(mult(me * cols + t * hc, hc), hc)] = hid.astype(BF16)
-
-    def pass_on(b, half_at, k, e, tt):
-        part = hidden.at[:, pl.ds(mult(b * cols + half_at * hc, hc), hc)]
-        go(remote(part, part, h_ss.at[k], h_rs.at[2 * b + half_at], e, tt))
-
-    def arrives(b, half_at):
-        part = hidden.at[:, pl.ds(mult(b * cols + half_at * hc, hc), hc)]
-        remote(part, part, h_ss.at[0], h_rs.at[2 * b + half_at], mate, t).wait_recv()
-
-    for k in range(1, nz):
-        pass_on(me, t, k, zpeer(k), t)
-    pass_on(me, t, nz, me, ot)
-    pass_on(me, t, 0, mate, t)
-    for k in range(1, nz):
-        b = zpeer(k)
-        arrives(b, t)
-        pass_on(b, t, nz + k, me, ot)
-        pass_on(b, t, 2 * nz + k, mate, t)
-    for k in range(nz):
-        b = zpeer(k)
-        arrives(b, ot)
-        pass_on(b, ot, 3 * nz + k, mate, t)
-    for k in range(nz):
-        other = lax.rem(z + k, nz) * 2 + 1 - c
-        arrives(other, t)
-        arrives(other, ot)
+
+    def y_copy(st):
+        rows = slice(*stages[st])
+        return remote(
+            ybuf.at[rows, there], yrecv.at[rows], y_ss.at[st], y_rs.at[st], me, ot
+        )
+
+    def project(st):
+        first, last = stages[st]
+        for at in range(first // (2 * tokens), last // (2 * tokens)):
+            b = (at + 1) % nz * 2 + 1 - c
+            block = attn.at[slot(b)]
+            remote(block, block, m_up_ss.at[0], m_up_rs.at[slot(b)], mate, t).wait_recv()
+        rows = slice(first, last)
+        lhs = attn[first // tokens : last // tokens].reshape(last - first, heads_cols)
+        ybuf[rows] = dot(lhs, wo[...]).astype(BF16)
+        go(y_copy(st))
+
+    def pass_on(st, b, half_at, k, e, tt):
+        rows = slice(*stages[st])
+        part = hidden.at[rows, pl.ds(mult(b * cols + half_at * hc, hc), hc)]
+        at = 4 * nz * st + k
+        go(remote(part, part, h_ss.at[at], h_rs.at[2 * n * st + 2 * b + half_at], e, tt))
+
+    def arrives(st, b, half_at):
+        rows = slice(*stages[st])
+        part = hidden.at[rows, pl.ds(mult(b * cols + half_at * hc, hc), hc)]
+        remote(
+            part, part, h_ss.at[0], h_rs.at[2 * n * st + 2 * b + half_at], mate, t
+        ).wait_recv()
+
+    def finish(st):
+        rows = slice(*stages[st])
+        y_copy(st).wait_recv()
+        hid = sorted_resid[rows].astype(F32) + (
+            ybuf[rows, here].astype(F32) + yrecv[rows].astype(F32)
+        )
+        hidden[rows, pl.ds(mult(me * cols + t * hc, hc), hc)] = hid.astype(BF16)
+        for k in range(1, nz):
+            pass_on(st, me, t, k, zpeer(k), t)
+        pass_on(st, me, t, nz, me, ot)
+        pass_on(st, me, t, 0, mate, t)
+
+    near_first = list(range(nz - 1, 0, -1))
+
+    def relay_z(st):
+        for k in near_first:
+            b = zpeer(k)
+            arrives(st, b, t)
+            pass_on(st, b, t, nz + k, me, ot)
+            pass_on(st, b, t, 2 * nz + k, mate, t)
+
+    def relay_x(st):
+        for k in [0, *near_first]:
+            b = zpeer(k)
+            arrives(st, b, ot)
+            pass_on(st, b, ot, 3 * nz + k, mate, t)
+
+    def from_mates(st):
+        for k in [0, *near_first]:
+            other = zline(k) * 2 + 1 - c
+            arrives(st, other, t)
+            arrives(st, other, ot)
+
+    def expert(st):
+        rows = slice(*stages[st])
+        for x in range(experts_here):
+            mix = mixes[rows, 3 * x : 3 * x + 1] + (
+                mixes[rows, 3 * x + 1 : 3 * x + 2] + mixes[rows, 3 * x + 2 : 3 * x + 3]
+            )
+            gate = dot(hidden[rows], wg[x])
+            value = gate / (1.0 + jnp.exp(-gate)) * dot(hidden[rows], wu[x]) * mix
+            act[rows, x * ff : (x + 1) * ff] = value.astype(BF16)
+
+    for d in range(1, nz - 1):
+        take(d)
+    loads[0].wait()
+    project(0)
+    take(nz - 1)
+    project(1)
+    for k in range(1, n):
+        e = peer(k)
+        remote(resid.at[e], resid.at[e], r_ss.at[k], r_rs.at[e], e, t).wait_recv()
+    sorted_resid[...] = dot(to_sorted, resid[...].reshape(everyone, hc)).astype(BF16)
+    finish(0)
+    finish(1)
+    relay_z(0)
+    relay_z(1)
+    relay_x(0)
+    from_mates(0)
     loads[1].wait()
     loads[2].wait()
-    for x in range(experts_here):
-        gate = dot(hidden[...], wg[x])
-        value = gate / (1.0 + jnp.exp(-gate)) * dot(hidden[...], wu[x]) * mixes[x]
-        act[:, x * ff : (x + 1) * ff] = value.astype(BF16)
+    expert(0)
+    relay_x(1)
+    from_mates(1)
+    expert(1)
     loads[3].wait()
-
-    order = [*range(1, nz), 0]
-
-    def down(side, at_sem):
-        at_cols = pl.ds(mult(side * half, half), half)
+    there = pl.ds(mult(ot * half, half), half)
+    here = pl.ds(mult(t * half, half), half)
+    pair = 2 * tokens
+    chunks = [(0, nz // 2), (nz // 2, nz)]
+
+    def down(at_cols, at_sem, chunk):
+        first, last = chunk
+        rows = slice(first * pair, last * pair)
         part = None
         for x in range(experts_here):
-            term = dot(act[:, x * ff : (x + 1) * ff], wd[x, :, at_cols])
+            term = dot(own_act[rows, x * ff : (x + 1) * ff], wd[x, :, at_cols])
             part = term if part is None else part + term
-        total[:, at_cols] = part
-        for k in order:
-            zz = lax.rem(z + k, nz)
+        total[rows, at_cols] = part
+        for zz in range(first, last):
             theirs = pl.ds(mult((zz * 2 + 1 - c) * tokens, tokens), tokens)
             dsend[zz, :, at_cols] = total[theirs, at_cols].astype(BF16)
             moved = dsend.at[zz, :, at_cols]
             dest = drecv.at[zz, :, at_cols]
-            go(remote(moved, dest, d_ss.at[at_sem + k], d_rs.at[at_sem + zz], mate, t))
-
-    def from_mate(side, at_sem, k, zz):
-        at_cols = pl.ds(mult(side * half, half), half)
+            go(remote(moved, dest, d_ss.at[at_sem + zz], d_rs.at[at_sem + zz], mate, t))
+
+    def from_mate(at_cols, at_sem, zz):
         dest = drecv.at[zz, :, at_cols]
-        remote(dest, dest, d_ss.at[at_sem + k], d_rs.at[at_sem + zz], mate, t).wait_recv()
-
-    down(ot, 0)
-    there = pl.ds(mult(ot * half, half), half)
-    here = pl.ds(mult(t * half, half), half)
-    for k in order:
-        zz = lax.rem(z + k, nz)
-        from_mate(ot, 0, k, zz)
-        ours = pl.ds(mult((zz * 2 + c) * tokens, tokens), tokens)
-        xsend[zz] = (total[ours, there] + drecv[zz, :, there].astype(F32)).astype(BF16)
-        go(remote(xsend.at[zz], xrecv.at[zz], x_ss.at[k], x_rs.at[zz], me, ot))
-    down(t, nz)
-    for k in order:
-        zz = lax.rem(z + k, nz)
-        from_mate(t, nz, k, zz)
-        remote(xsend.at[zz], xrecv.at[zz], x_ss.at[k], x_rs.at[zz], me, ot).wait_recv()
-        ours = pl.ds(mult((zz * 2 + c) * tokens, tokens), tokens)
-        done = total[ours, here] + drecv[zz, :, here].astype(F32) + xrecv[zz].astype(F32)
-        if k:
-            zsend[zz] = done.astype(BF16)
-            go(remote(zsend.at[zz], zrecv.at[z], z_ss.at[k], z_rs.at[z], zz * 2 + c, t))
-        else:
-            total[ours, here] = done
+        remote(dest, dest, d_ss.at[at_sem + zz], d_rs.at[at_sem + zz], mate, t).wait_recv()
+
+    def ours(zz):
+        return pl.ds(mult((zz * 2 + c) * tokens, tokens), tokens)
+
+    def to_x(chunk):
+        for zz in range(*chunk):
+            from_mate(there, 0, zz)
+            xsend[zz] = (total[ours(zz), there] + drecv[zz, :, there].astype(F32)).astype(BF16)
+            go(remote(xsend.at[zz], xrecv.at[zz], x_ss.at[zz], x_rs.at[zz], me, ot))
+
+    for i, chunk in enumerate(chunks):
+        rows = slice(chunk[0] * pair, chunk[1] * pair)
+        own_act[rows] = dot(perm[rows], act[...]).astype(BF16)
+        down(there, 0, chunk)
+    down(here, nz, chunks[0])
+    to_x(chunks[0])
+    down(here, nz, chunks[1])
+    to_x(chunks[1])
+    for zz in range(nz):
+        from_mate(here, nz, zz)
+        remote(xsend.at[zz], xrecv.at[zz], x_ss.at[zz], x_rs.at[zz], me, ot).wait_recv()
+        done = total[ours(zz), here] + drecv[zz, :, here].astype(F32) + xrecv[zz].astype(F32)
+        zsend[zz] = done.astype(BF16)
+        total[ours(zz), here] = done
+
+        def send_on(zz=zz):
+            remote(
+                zsend.at[zz], zrecv.at[z], z_ss.at[zz], z_rs.at[z], zz * 2 + c, t
+            ).start()
+
+        pl.when(z != zz)(send_on)
     own_rows = pl.ds(mult(me * tokens, tokens), tokens)
-    final = total[own_rows, pl.ds(mult(t * half, half), half)]
-    final = final + hidden[own_rows, here].astype(F32)
+    final = total[own_rows, here] + dot(perm[own_rows], hidden[:, here])
+    for off, way, copy in predicated:
+        pl.when(inside_line(z + off) & inside_line(z + way))(lambda copy=copy: copy().wait_send())
+    for copy in sends:
+        copy.wait_send()
     for k in range(1, nz):
         zz = lax.rem(z + k, nz)
-        remote(zsend.at[zz], zrecv.at[zz], z_ss.at[k], z_rs.at[zz], zz * 2 + c, t).wait_recv()
+        remote(zrecv.at[zz], zrecv.at[zz], z_ss.at[0], z_rs.at[zz], zz * 2 + c, t).wait_recv()
         final = final + zrecv[zz].astype(F32)
     out[...] = final.astype(BF16)
-    for copy in sends:
-        copy.wait_send()
+    for zz in range(nz):
+
+        def sent(zz=zz):
+            remote(
+                zsend.at[zz], zrecv.at[z], z_ss.at[zz], z_rs.at[z], zz * 2 + c, t
+            ).wait_send()
+
+        pl.when(z != zz)(sent)
 
 
 def fused(
@@ -628,9 +794,15 @@
     return pl.pallas_call(
         functools.partial(fused_kernel, (n, tokens, per, kvl, group)),
         out_shape=jax.ShapeDtypeStruct((tokens, half), BF16),
-        in_specs=[vspec] * 8 + [hspec] * 4,
+        in_specs=[hspec] * 12,
         out_specs=vspec,
         scratch_shapes=[
+            vm(queries.shape),
+            vm(own_kv.shape),
+            vm((1, 1), jnp.int32),
+            vm((1, tokens), jnp.int32),
+            vm(route_ids.shape[::-1], jnp.int32),
+            vm(route_weights.shape[::-1], F32),
             vm(out_weight.shape),
             vm(w_gate.shape),
             vm(w_up.shape),
@@ -641,10 +813,14 @@
             vm((n, 8, HD), F32),
             vm((n, 8, HD), F32),
             vm((n, tokens, cols // 2)),
+            vm((every, cols // 2)),
+            vm((every, every)),
+            vm((every, HD), F32),
             vm((n, tokens, kvl * group * HD)),
             vm((every, cols)),
             vm((every, cols // 2)),
             vm((every, model)),
+            vm((every, x_here * ff)),
             vm((every, x_here * ff)),
             vm((every, model), F32),
             vm((nz, tokens, model)),
@@ -653,6 +829,7 @@
             vm((nz, tokens, half)),
             vm((nz, tokens, half)),
             vm((nz, tokens, half)),
+            sem((9,)),
             sem((4,)),
             sem((n,)),
             sem((n,)),
@@ -662,12 +839,14 @@
             sem((n,)),
             sem((2,)),
             sem((2,)),
+            sem((4 * kvl * nz,)),
+            sem((2 * kvl * n,)),
             sem((2 * nz,)),
             sem((n,)),
-            sem((1,)),
-            sem((1,)),
-            sem((4 * nz,)),
-            sem((2 * n,)),
+            sem((2,)),
+            sem((2,)),
+            sem((8 * nz,)),
+            sem((4 * n,)),
             sem((2 * nz,)),
             sem((2 * nz,)),
             sem((nz,)),
@@ -702,6 +881,7 @@
     fits = (
         lax.axis_size("tensor") == 2
         and n % 2 == 0
+        and n >= 8
         and tokens % 16 == 0
         and tokens <= HD
         and tokens % (n // 2) == 0

time: 66.6 us -> 58.7 us (0.88)
  the two profiles are of different devices: /device:TPU:0 before, /device:TPU:24 now
where the time goes in v1:
time: 58.7 us; the launch traced here: 58.5 us
  Pallas kernels  56.4 us (96%)
  local copies, waits for them, and re-layouts  1.47 us (3%)
  between operations  0.66 us (1%)
    pallas_call x1, Pallas kernels, fused(): pl.pallas_call(functools.partial(fused_kernel, (n, tokens, per, kvl, grou...  56.4 us
    unnamed x1, local copies, waits for them, and re-layouts  1.47 us

profile of v1, /device:TPU:24, one launch (start us, length us, event | category | flops | bytes accessed | tf_op | source)
XLA Modules:
  0.0 58.5 jit_solution(3806816805885225075)
XLA Ops:
  0.7 56.4 %shard_map.118 = bf16[32,1024]{1,0:T(8,128)(2,1)} custom-call(bf16[32,4096]{1,0:T(8,128)(2,1)} %queries_hbm.1, bf16[32,1024]{1,0:T(8,128)(2,1)} %own_kv_hbm.1, bf16[1,128,1024]{2,1,0:T(8,128)(2,1)} %cache.1, s32[1,1]{1,0:T(1,128)} %bitcast.4.length_hbm, s32[1,32]{1,0:T(1,128)} %bitcast.7, bf16[32,2048]{1,0:T(8,128)(2,1)} %residual.1, s32[8,32]{1,0:T(8,128)} %bitcast.5, ...), custom_call_target="tpu_custom_call" | custom-call | tf_op jit(solution)/shard_map/pallas_call | solution.py:794
  57.0 1.5 %copy.15 = bf16[32,1024]{1,0:T(8,128)(2,1)} copy(bf16[32,1024]{1,0:T(8,128)(2,1)} %shard_map.118) | data formatting | bytes 131072
